TPU v7x, 128 devices: a whole 4x4x4 slice. The times are simulated.
128 devices in a mesh: dp: 16 (over x_lo, z, core), expert: 8 (over y, x_hi).
Axes of the slice: x: 4 (x_hi: 2, x_lo: 2; x = x_hi * 2 + x_lo), y: 4, z: 4, core: 2. Of those that a mesh axis runs over, the one named last changes fastest.
Arguments:
- tokens: bfloat16 [16384, 2048], P(('dp', 'expert')), may hold values from -6 to 6
- norm_gain: float32 [2048], replicated, may hold values from 0.25 to 1.75
- router_weight: bfloat16 [2048, 64], P('dp'), may hold values from -0.25 to 0.25
- expert_ids: int32 [16384, 8], P(('dp', 'expert')), may hold values from 0 to 63, all different within a row; in each aligned block of 128 rows (0 to 127, 128 to 255, ...) at most 32 rows name the same one
- gate_weight: bfloat16 [8, 2048, 1024], P('expert', 'dp'), may hold values from -0.125 to 0.125
- up_weight: bfloat16 [8, 2048, 1024], P('expert', 'dp'), may hold values from -0.125 to 0.125
- down_weight: bfloat16 [8, 2048, 1024], P('expert', 'dp'), may hold values from -0.1875 to 0.1875
- cotangent: bfloat16 [16384, 2048], P(('dp', 'expert')), may hold values from -6 to 6
Outputs:
- mixed: bfloat16 [16384, 2048], P(('dp', 'expert'))
- d_tokens: bfloat16 [16384, 2048], P(('dp', 'expert'))
- d_gain: float32 [2048], replicated
- d_router: float32 [2048, 64], P('dp')
- d_gate: bfloat16 [8, 2048, 1024], P('expert', 'dp')
- d_up: bfloat16 [8, 2048, 1024], P('expert', 'dp')
- d_down: bfloat16 [8, 2048, 1024], P('expert', 'dp')
Inputs may be any that keep to these rules, and one draw needn't show every extreme that they name: `expert_ids`: each row names 8 different experts; in the rows of one device no expert is named more than 32 times.
All inputs are finite; a program needn't handle non-finite values.
Results may differ from a plain program's by a relative error of at most 0.018.
Values may be sent and summed in bfloat16 or wider, within the bound.
No kernel may reach another device: no remote copies, remote signals or barrier semaphores. Data moves between devices by JAX's collectives and lax.ppermute only.
A program may use at most 128 MiB of HBM per device.

v0:
```python
import jax
import jax.numpy as jnp
from jax import lax
from jax.sharding import PartitionSpec as P

D = 2048
FF = 1024
CAP = 32
EPSILON = 1e-05
HIGHEST = lax.Precision.HIGHEST


def in_one_piece(arrays, axis, dim, along):
    both = jnp.concatenate(arrays, axis=along)
    result, at, finished = (lax.all_gather(both, axis, axis=dim, tiled=True), 0, [])
    for a in arrays:
        finished.append(lax.slice_in_dim(result, at, at + a.shape[along], axis=along))
        at += a.shape[along]
    return tuple(finished)


def split_up(x, dim, length):
    shape = x.shape
    pieces = x.reshape(*shape[:dim], length, shape[dim] // length, *shape[dim + 1 :])
    return jnp.moveaxis(pieces, dim, 0)


def sum_at_owner(x, axis, dim):
    length = lax.axis_size(axis)
    pieces = lax.all_to_all(split_up(x, dim, length), axis, 0, 0, tiled=True)
    return jnp.sum(pieces.astype(jnp.float32), axis=0)


def copy_for_each(x, axis):
    copies = jnp.broadcast_to(x, (lax.axis_size(axis), *x.shape))
    return lax.all_to_all(copies, axis, split_axis=0, concat_axis=0, tiled=True)


def over_copies(x, axis):
    everything = copy_for_each(x, axis)
    return jnp.sum(everything.astype(jnp.float32), axis=0)


def normalize(inputs, norm_gain):
    meansq = jnp.mean(inputs * inputs, axis=-1, keepdims=True)
    return inputs * lax.rsqrt(meansq + EPSILON) * norm_gain


def gate_weights(logits, expert_ids):
    member = (
        expert_ids[:, :, None] == jnp.arange(logits.shape[-1], dtype=jnp.int32)[None, None, :]
    ).astype(jnp.float32)
    picked = jnp.sum(member * logits[:, None, :], axis=-1)
    raised = jnp.exp(picked)
    return raised / jnp.sum(raised, axis=-1, keepdims=True)


def pick_matrix(expert_ids, window, capacity):
    flat_ids = expert_ids.reshape(-1)
    chosen = (flat_ids[:, None] == jnp.arange(window, dtype=jnp.int32)[None, :]).astype(jnp.int32)
    before = jnp.cumsum(chosen, axis=0, dtype=jnp.int32) - chosen
    position = jnp.sum(before * chosen, axis=-1)
    target = jnp.where(flat_ids < window, flat_ids * capacity + position, -1)
    columns = jnp.arange(window * capacity, dtype=jnp.int32)
    matrix = (target[:, None] == columns[None, :]).astype(jnp.float32)
    return matrix.reshape(expert_ids.shape[0], expert_ids.shape[1], window * capacity)


def expert_forward(slot_rows, w_gate, w_up, w_down):
    gate_pre = jnp.dot(slot_rows, w_gate, preferred_element_type=jnp.float32)
    up_pre = jnp.dot(slot_rows, w_up, preferred_element_type=jnp.float32)
    active = (gate_pre * jax.nn.sigmoid(gate_pre) * up_pre).astype(jnp.bfloat16)
    output = jnp.dot(active, w_down.T, preferred_element_type=jnp.float32).astype(jnp.bfloat16)
    return (output, gate_pre, up_pre)


def expert_backward(slot_grads, gate_pre, up_pre, w_gate, w_up, w_down):
    sigmoid_gate = jax.nn.sigmoid(gate_pre)
    active = (gate_pre * sigmoid_gate * up_pre).astype(jnp.bfloat16)
    back = jnp.dot(slot_grads, w_down, preferred_element_type=jnp.float32)
    grad_gate = (back * up_pre * sigmoid_gate * (1.0 + gate_pre * (1.0 - sigmoid_gate))).astype(
        jnp.bfloat16
    )
    grad_upper = (back * gate_pre * sigmoid_gate).astype(jnp.bfloat16)
    grad_rows = jnp.dot(grad_gate, w_gate.T, preferred_element_type=jnp.float32)
    grad_rows = (
        grad_rows + jnp.dot(grad_upper, w_up.T, preferred_element_type=jnp.float32)
    ).astype(jnp.bfloat16)
    return (grad_rows, active, grad_gate, grad_upper)


def body(
    tokens, norm_gain, router_weight, expert_ids, gate_weight, up_weight, down_weight, cotangent
):
    window = lax.axis_size("expert")
    slot_count = window * CAP
    router_full = lax.all_gather(router_weight, "dp", axis=0, tiled=True)
    inputs = tokens.astype(jnp.float32)
    hidden = normalize(inputs, norm_gain).astype(jnp.bfloat16)
    logits = jnp.dot(hidden, router_full, preferred_element_type=jnp.float32)
    weights, gate_back = jax.vjp(lambda values: gate_weights(values, expert_ids), logits)
    pick_table = pick_matrix(expert_ids, window, CAP)
    spread_half = jnp.sum(pick_table, axis=1).astype(jnp.bfloat16)
    blending = jnp.einsum("tks,tk->ts", pick_table, weights, precision=HIGHEST)
    outgoing = (
        jnp.dot(spread_half.T, hidden, preferred_element_type=jnp.float32)
        .astype(jnp.bfloat16)
        .reshape(window, CAP, D)
    )
    weights_full = in_one_piece((gate_weight, up_weight, down_weight), "dp", 1, 0)
    w_gate = weights_full[0][0]
    w_up = weights_full[1][0]
    w_down = weights_full[2][0]
    arrived_rows = lax.all_to_all(outgoing, "expert", split_axis=0, concat_axis=0, tiled=True)
    lead = arrived_rows.shape[0]
    middle = arrived_rows.shape[1]
    output, gate_pre, up_pre = expert_forward(arrived_rows.reshape(-1, D), w_gate, w_up, w_down)
    produced = output.reshape(lead, middle, D)
    gate_slots = gate_pre.reshape(lead, middle, FF)
    upper_slots = up_pre.reshape(lead, middle, FF)
    returned = lax.all_to_all(produced, "expert", split_axis=0, concat_axis=0, tiled=True).reshape(
        slot_count, D
    )
    returned_wide = returned.astype(jnp.float32)
    mixed_out = jnp.dot(blending, returned_wide, precision=HIGHEST).astype(jnp.bfloat16)
    gathered_cot = jnp.dot(spread_half.T, cotangent, preferred_element_type=jnp.float32)
    per_slot = jnp.sum(gathered_cot * returned_wide, axis=-1)
    grad_weights = jnp.einsum("tks,s->tk", pick_table, per_slot, precision=HIGHEST)
    grad_logits = gate_back(grad_weights)[0]
    outgoing_grad = (
        jnp.dot(blending.T, cotangent.astype(jnp.float32), precision=HIGHEST)
        .astype(jnp.bfloat16)
        .reshape(window, CAP, D)
    )
    arrived_grad = lax.all_to_all(outgoing_grad, "expert", split_axis=0, concat_axis=0, tiled=True)
    flat_rows = arrived_rows.reshape(-1, D)
    flat_grads = arrived_grad.reshape(-1, D)
    grad_rows, active, grad_gate, grad_upper = expert_backward(
        flat_grads, gate_slots.reshape(-1, FF), upper_slots.reshape(-1, FF), w_gate, w_up, w_down
    )
    grad_back = lax.all_to_all(
        grad_rows.reshape(window, CAP, D), "expert", split_axis=0, concat_axis=0, tiled=True
    ).reshape(slot_count, D)
    term_gate = jnp.dot(flat_rows.T, grad_gate, preferred_element_type=jnp.float32)
    term_upper = jnp.dot(flat_rows.T, grad_upper, preferred_element_type=jnp.float32)
    term_down = jnp.dot(flat_grads.T, active, preferred_element_type=jnp.float32)
    summed = lax.psum_scatter(
        jnp.concatenate([term_gate, term_upper, term_down], axis=1).astype(jnp.bfloat16),
        "dp",
        scatter_dimension=0,
        tiled=True,
    ).astype(jnp.float32)
    grad_hidden = jnp.dot(spread_half, grad_back, preferred_element_type=jnp.float32)
    grad_hidden = grad_hidden + jnp.dot(
        grad_logits, router_full.astype(jnp.float32).T, precision=HIGHEST
    )
    unused_value, norm_back = jax.vjp(normalize, inputs, norm_gain)
    grad_inputs, grad_gain = norm_back(grad_hidden)
    grad_router = jnp.dot(hidden.astype(jnp.float32).T, grad_logits, precision=HIGHEST)
    router_part = sum_at_owner(grad_router.astype(jnp.bfloat16), "dp", 0)
    router_mine = over_copies(router_part.astype(jnp.bfloat16), "expert").astype(jnp.float32)
    gain_sum = lax.psum(grad_gain, ("dp", "expert"))
    grad_gate_out = summed[:, :FF].astype(jnp.bfloat16)[None]
    grad_up_out = summed[:, FF : 2 * FF].astype(jnp.bfloat16)[None]
    grad_down_out = summed[:, 2 * FF :].astype(jnp.bfloat16)[None]
    return (
        mixed_out,
        grad_inputs.astype(jnp.bfloat16),
        gain_sum,
        router_mine,
        grad_gate_out,
        grad_up_out,
        grad_down_out,
    )


def solution(mesh):
    in_specs = (
        P(("dp", "expert"), None),
        P(),
        P("dp", None),
        P(("dp", "expert"), None),
        P("expert", "dp", None),
        P("expert", "dp", None),
        P("expert", "dp", None),
        P(("dp", "expert"), None),
    )
    out_specs = (
        P(("dp", "expert"), None),
        P(("dp", "expert"), None),
        P(),
        P("dp", None),
        P("expert", "dp", None),
        P("expert", "dp", None),
        P("expert", "dp", None),
    )
    return jax.shard_map(body, mesh=mesh, in_specs=in_specs, out_specs=out_specs, check_vma=False)
```

profile of v0, /device:TPU:1, one launch (start us, length us, event | category | flops | bytes accessed | tf_op | source)
XLA Modules:
  0.0 330.0 jit_solution(3319858266487233548)
XLA Ops:
  7.3 2.2 pad_maximum_fusion.1
  9.5 0.8 copy.56
  10.4 2.3 reduce-window.6
  13.4 0.7 add_select_fusion
  14.2 0.4 convert_reduce_fusion
  14.6 1.2 fusion.16
  15.9 2.5 convolution_convert_fusion.3
  18.4 7.5 %all-to-all-start = ((bf16[8,32,2048]{2,1,0:T(8,128)(2,1)}), bf16[8,32,2048]{2,1,0:T(8,128)(2,1)S(1)}, u32[]{:S(2)}, u32[]{:S(2)}) async-start(bf16[8,32,2048]{2,1,0:T(8,128)(2,1)} %bitcast.3), calls=%async_computation | async-start | bytes 2097152 | tf_op jit(solution)/shard_map/all_to_all | solution.py:114
  25.9 41.0 %all_gather.6 = bf16[2048,64]{0,1:T(8,128)(2,1)S(1)} all-gather(bf16[128,64]{0,1:T(8,128)(2,1)S(1)} %copy-done.14), channel_id=1, replica_groups=mesh['dp'=16,'expert'=8] {'dp'}, dimensions={0}, use_global_device_ids=true | all-gather | bytes 278528 | tf_op jit(solution)/shard_map/all_gather | solution.py:97
  67.0 0.7 copy-done.2
  68.2 0.7 fusion.19
  69.0 2.1 convolution_convert_fusion.4
  71.1 6.8 %all-to-all-start.2 = ((bf16[8,32,2048]{2,1,0:T(8,128)(2,1)}), bf16[8,32,2048]{2,1,0:T(8,128)(2,1)S(1)}, u32[]{:S(2)}, u32[]{:S(2)}) async-start(bf16[8,32,2048]{2,1,0:T(8,128)(2,1)} %bitcast.109), calls=%async_computation.2 | async-start | bytes 2097152 | tf_op jit(solution)/shard_map/all_to_all | solution.py:135
  78.1 30.4 %all-gather.2.cloned.1.call-done = bf16[3,2048,1024]{2,1,0:T(8,128)(2,1)} async-done(((bf16[3,128,1024]{2,1,0:T(8,128)(2,1)}), bf16[3,2048,1024]{2,1,0:T(8,128)(2,1)}) %all-gather.2.cloned.1.call-update) | async-done | bytes 12582928 | tf_op jit(solution)/shard_map/all_gather | solution.py:15
  108.5 4.4 %fusion.3 = f32[256,1024]{1,0:T(8,128)} fusion(bf16[256,2048]{1,0:T(8,128)(2,1)S(1)} %bitcast.100, bf16[3,2048,1024]{2,1,0:T(8,128)(2,1)} %all-gather.2.cloned.1.call-done), kind=kOutput, calls=%fused_computation.10 | convolution fusion | flops 1073741824 | bytes 6291456 | tf_op jit(solution)/shard_map/dot_general | solution.py:71
  112.9 4.4 %fusion.1 = f32[256,1024]{1,0:T(8,128)} fusion(bf16[256,2048]{1,0:T(8,128)(2,1)S(1)} %bitcast.101, bf16[3,2048,1024]{2,1,0:T(8,128)(2,1)} %all-gather.2.cloned.1.call-done), kind=kOutput, calls=%fused_computation.8 | convolution fusion | flops 1073741824 | bytes 6291456 | tf_op jit(solution)/shard_map/dot_general | solution.py:70
  117.3 4.4 %multiply_convert_fusion = (bf16[256,1024]{1,0:T(8,128)(2,1)S(1)}, bf16[256,1024]{1,0:T(8,128)(2,1)S(1)}, bf16[256,1024]{1,0:T(8,128)(2,1)S(1)}) fusion(f32[256,1024]{1,0:T(8,128)} %fusion.1, f32[256,1024]{1,0:T(8,128)} %fusion.3, bf16[256,2048]{1,0:T(8,128)(2,1)S(1)} %bitcast.104, bf16[3,2048,1024]{2,1,0:T(8,128)(2,1)} %all-gather.2.cloned.1.call-done), kind=kOutput, calls=%fused_computation.36 | convolution fusion | flops 1077936128 | bytes 8912896 | tf_op jit(solution)/shard_map/dot_general | solution.py:80
  121.7 1.3 convolution_convert_fusion
  123.1 1.3 convolution_convert_fusion.1
  124.4 1.3 convolution_convert_fusion.2
  125.7 21.2 %pad_maximum_fusion = bf16[2048,3072]{0,1:T(8,128)(2,1)} fusion(bf16[2048,1024]{0,1:T(8,128)(2,1)S(1)} %convolution_convert_fusion, bf16[2048,1024]{0,1:T(8,128)(2,1)S(1)} %convolution_convert_fusion.1, bf16[2048,1024]{0,1:T(8,128)(2,1)S(1)} %convolution_convert_fusion.2), kind=kLoop, calls=%fused_computation | loop fusion | flops 37748736 | bytes 25165824 | tf_op jit(solution)/shard_map/concatenate | solution.py:148
  146.9 16.6 %copy.68 = bf16[2048,3072]{1,0:T(8,128)(2,1)} copy(bf16[2048,3072]{0,1:T(8,128)(2,1)} %pad_maximum_fusion) | data formatting | bytes 25165824
  163.6 1.0 copy-done.8
  164.6 4.6 %fusion.8 = bf16[256,2048]{1,0:T(8,128)(2,1)} fusion(bf16[256,1024]{1,0:T(8,128)(2,1)S(1)} %copy-done.8, bf16[3,2048,1024]{2,1,0:T(8,128)(2,1)} %all-gather.2.cloned.1.call-done), kind=kOutput, calls=%fused_computation.17 | convolution fusion | flops 1074266112 | bytes 5767168 | tf_op jit(solution)/shard_map/dot_general | solution.py:73
  169.2 6.1 %all-to-all-start.1 = ((bf16[8,32,2048]{2,1,0:T(8,128)(2,1)}), bf16[8,32,2048]{2,1,0:T(8,128)(2,1)S(1)}, u32[]{:S(2)}, u32[]{:S(2)}) async-start(bf16[8,32,2048]{2,1,0:T(8,128)(2,1)} %bitcast.8), calls=%async_computation.1 | async-start | bytes 2097152 | tf_op jit(solution)/shard_map/all_to_all | solution.py:121
  175.3 3.5 %fusion = f32[256,2048]{1,0:T(8,128)S(1)} fusion(bf16[256,1024]{1,0:T(8,128)(2,1)S(1)} %copy-done.6, bf16[3,2048,1024]{2,1,0:T(8,128)(2,1)} %all-gather.2.cloned.1.call-done), kind=kOutput, calls=%fused_computation.7 | convolution fusion | flops 1073741824 | bytes 6815744 | tf_op jit(solution)/shard_map/dot_general | solution.py:85
  178.9 4.5 %fusion.7 = bf16[256,2048]{1,0:T(8,128)(2,1)} fusion(f32[256,2048]{1,0:T(8,128)S(1)} %fusion, bf16[256,1024]{1,0:T(8,128)(2,1)S(1)} %copy-done.4, bf16[3,2048,1024]{2,1,0:T(8,128)(2,1)} %all-gather.2.cloned.1.call-done), kind=kOutput, calls=%fused_computation.16 | convolution fusion | flops 1074790400 | bytes 7864320 | tf_op jit(solution)/shard_map/dot_general | solution.py:87
  183.4 14.9 %all-to-all-done.1 = bf16[8,32,2048]{2,1,0:T(8,128)(2,1)S(1)} async-done(((bf16[8,32,2048]{2,1,0:T(8,128)(2,1)}), bf16[8,32,2048]{2,1,0:T(8,128)(2,1)S(1)}, u32[]{:S(2)}, u32[]{:S(2)}) %all-to-all-start.1) | async-done | bytes 1048608 | tf_op jit(solution)/shard_map/all_to_all | solution.py:121
  198.3 3.6 %all-to-all-start.3 = ((bf16[8,32,2048]{2,1,0:T(8,128)(2,1)}), bf16[8,32,2048]{2,1,0:T(8,128)(2,1)S(1)}, u32[]{:S(2)}, u32[]{:S(2)}) async-start(bf16[8,32,2048]{2,1,0:T(8,128)(2,1)} %bitcast.110), calls=%async_computation.3 | async-start | bytes 2097152 | tf_op jit(solution)/shard_map/all_to_all | solution.py:141
  201.8 0.5 fusion.9
  202.4 3.6 %fusion.18 = f32[1,128,8]{2,0,1:T(1,128)S(1)} fusion(f32[256,1,1]{0,1,2:T(1,128)S(1)} %bitcast.115, s32[128,8]{1,0:T(8,128)S(1)} %copy.59), kind=kOutput, calls=%fused_computation.42 | convolution fusion | flops 3407872 | bytes 9216 | tf_op jit(solution)/shard_map/tks,s->tk/dot_general | solution.py:128
  206.2 0.5 fusion.12
  206.8 0.8 copy.86
  207.6 16.8 %all-to-all-done.3 = bf16[8,32,2048]{2,1,0:T(8,128)(2,1)S(1)} async-done(((bf16[8,32,2048]{2,1,0:T(8,128)(2,1)}), bf16[8,32,2048]{2,1,0:T(8,128)(2,1)S(1)}, u32[]{:S(2)}, u32[]{:S(2)}) %all-to-all-start.3) | async-done | bytes 1048608 | tf_op jit(solution)/shard_map/all_to_all | solution.py:141
  224.4 6.8 %all-to-all-start.4 = ((bf16[16,128,64]{1,2,0:T(8,128)(2,1)}), bf16[16,128,64]{1,2,0:T(8,128)(2,1)S(1)}, u32[]{:S(2)}, u32[]{:S(2)}) async-start(bf16[16,128,64]{1,2,0:T(8,128)(2,1)} %bitcast.98), calls=%async_computation.4 | async-start | bytes 524288 | tf_op jit(solution)/shard_map/all_to_all | solution.py:30
  231.5 1.9 fusion.14
  233.4 0.6 multiply_multiply_fusion
  234.1 1.1 fusion.15
  235.2 5.1 %all-to-all-done.4 = bf16[16,128,64]{1,2,0:T(8,128)(2,1)S(1)} async-done(((bf16[16,128,64]{1,2,0:T(8,128)(2,1)}), bf16[16,128,64]{1,2,0:T(8,128)(2,1)S(1)}, u32[]{:S(2)}, u32[]{:S(2)}) %all-to-all-start.4) | async-done | bytes 262176 | tf_op jit(solution)/shard_map/all_to_all | solution.py:30
  240.3 0.7 broadcast_in_dim.44
  241.0 3.4 %all-to-all-start.5 = ((bf16[8,128,64]{1,2,0:T(8,128)(2,1)}), bf16[8,128,64]{1,2,0:T(8,128)(2,1)S(1)}, u32[]{:S(2)}, u32[]{:S(2)}) async-start(bf16[8,128,64]{1,2,0:T(8,128)(2,1)} %broadcast_in_dim.44), calls=%async_computation.5 | async-start | bytes 262144 | tf_op jit(solution)/shard_map/all_to_all | solution.py:36
  244.4 1.4 convolution_convert_fusion.5
  245.8 72.5 %psum.7 = f32[2048]{0:T(1024)} all-reduce(f32[2048]{0:T(1024)S(1)} %get-tuple-element.42), channel_id=1, replica_groups=mesh['dp'=16,'expert'=8] {'dp','expert'}, use_global_device_ids=true, to_apply=%region_12.13 | all-reduce | flops 2048 | bytes 16384 | tf_op jit(solution)/shard_map/psum | solution.py:162
  318.3 0.6 convert_reduce_fusion.1
  318.9 1.2 fusion.43
  320.3 0.9 copy.64
  321.3 0.9 copy.63
  322.3 0.9 copy.62
  (69 shorter events, 3.0 us)
Async XLA Ops:
  7.2 61.8 %copy-start = (bf16[128,2048]{1,0:T(8,128)(2,1)S(1)}, bf16[128,2048]{1,0:T(8,128)(2,1)}, u32[]{:S(2)}) copy-start(bf16[128,2048]{1,0:T(8,128)(2,1)} %param.15) | copy-start | bytes 1572868
  7.2 60.9 %copy-start.13 = (s32[128,8]{0,1:T(8,128)S(1)}, s32[128,8]{0,1:T(8,128)}, u32[]{:S(2)}) copy-start(s32[128,8]{0,1:T(8,128)} %param.11) | copy-start | bytes 12292
  7.2 60.5 %copy-start.1 = (bf16[128,2048]{1,0:T(8,128)(2,1)S(1)}, bf16[128,2048]{1,0:T(8,128)(2,1)}, u32[]{:S(2)}) copy-start(bf16[128,2048]{1,0:T(8,128)(2,1)} %param.8) | copy-start | bytes 1572868
  7.2 60.5 %copy-start.12 = (f32[2048]{0:T(1024)S(1)}, f32[2048]{0:T(1024)}, u32[]{:S(2)}) copy-start(f32[2048]{0:T(1024)} %param.9) | copy-start | bytes 24580
  7.2 18.7 %copy-start.14 = (bf16[128,64]{0,1:T(8,128)(2,1)S(1)}, bf16[128,64]{0,1:T(8,128)(2,1)}, u32[]{:S(2)}) copy-start(bf16[128,64]{0,1:T(8,128)(2,1)} %param.10) | copy-start | bytes 49156
  7.2 101.3 %all-gather.2.cloned.1.call-start = ((), (), s32[]{:S(2)}) async-start(), calls=%async_computation.7 | async-start | bytes 13369344 | tf_op jit(solution)/shard_map/all_gather | solution.py:15
  15.9 10.0 %copy-start.17 = (f32[128]{0:T(128)}, f32[128]{0:T(128)S(1)}, u32[]{:S(2)}) copy-start(f32[128]{0:T(128)S(1)} %fusion.16) | copy-start | bytes 1540
  15.9 190.3 %copy-start.15 = (f32[128]{0:T(128)}, f32[128]{0:T(128)S(1)}, u32[]{:S(2)}) copy-start(f32[128]{0:T(128)S(1)} %fusion.34) | copy-start | bytes 1540
  18.4 52.6 %all-to-all-start = ((bf16[8,32,2048]{2,1,0:T(8,128)(2,1)}), bf16[8,32,2048]{2,1,0:T(8,128)(2,1)S(1)}, u32[]{:S(2)}, u32[]{:S(2)}) async-start(bf16[8,32,2048]{2,1,0:T(8,128)(2,1)} %bitcast.3), calls=%async_computation | async-start | bytes 2097152 | tf_op jit(solution)/shard_map/all_to_all | solution.py:114
  67.0 0.7 copy-start.2
  69.0 2.1 copy-start.9
  71.1 46.3 %all-to-all-start.2 = ((bf16[8,32,2048]{2,1,0:T(8,128)(2,1)}), bf16[8,32,2048]{2,1,0:T(8,128)(2,1)S(1)}, u32[]{:S(2)}, u32[]{:S(2)}) async-start(bf16[8,32,2048]{2,1,0:T(8,128)(2,1)} %bitcast.109), calls=%async_computation.2 | async-start | bytes 2097152 | tf_op jit(solution)/shard_map/all_to_all | solution.py:135
  77.9 241.0 %reduce-scatter.4.cloned.1.call-start = ((), (), s32[]{:S(2)}) async-start(), calls=%async_computation.8 | async-start | bytes 13369344
  121.7 1.4 copy-start.7
  121.7 1.4 copy-start.3
  121.7 2.7 copy-start.5
  163.5 1.0 copy-start.8
  164.6 10.7 %copy-start.6 = (bf16[256,1024]{1,0:T(8,128)(2,1)S(1)}, bf16[256,1024]{1,0:T(8,128)(2,1)}, u32[]{:S(2)}) copy-start(bf16[256,1024]{1,0:T(8,128)(2,1)} %copy-done.5) | copy-start | bytes 1572868
  169.2 29.1 %all-to-all-start.1 = ((bf16[8,32,2048]{2,1,0:T(8,128)(2,1)}), bf16[8,32,2048]{2,1,0:T(8,128)(2,1)S(1)}, u32[]{:S(2)}, u32[]{:S(2)}) async-start(bf16[8,32,2048]{2,1,0:T(8,128)(2,1)} %bitcast.8), calls=%async_computation.1 | async-start | bytes 2097152 | tf_op jit(solution)/shard_map/all_to_all | solution.py:121
  175.3 3.5 %copy-start.4 = (bf16[256,1024]{1,0:T(8,128)(2,1)S(1)}, bf16[256,1024]{1,0:T(8,128)(2,1)}, u32[]{:S(2)}) copy-start(bf16[256,1024]{1,0:T(8,128)(2,1)} %copy-done.3) | copy-start | bytes 1572868
  198.3 26.1 %all-to-all-start.3 = ((bf16[8,32,2048]{2,1,0:T(8,128)(2,1)}), bf16[8,32,2048]{2,1,0:T(8,128)(2,1)S(1)}, u32[]{:S(2)}, u32[]{:S(2)}) async-start(bf16[8,32,2048]{2,1,0:T(8,128)(2,1)} %bitcast.110), calls=%async_computation.3 | async-start | bytes 2097152 | tf_op jit(solution)/shard_map/all_to_all | solution.py:141
  206.2 0.6 copy-start.11
  224.4 15.9 %all-to-all-start.4 = ((bf16[16,128,64]{1,2,0:T(8,128)(2,1)}), bf16[16,128,64]{1,2,0:T(8,128)(2,1)S(1)}, u32[]{:S(2)}, u32[]{:S(2)}) async-start(bf16[16,128,64]{1,2,0:T(8,128)(2,1)} %bitcast.98), calls=%async_computation.4 | async-start | bytes 524288 | tf_op jit(solution)/shard_map/all_to_all | solution.py:30
  231.2 2.9 copy-start.16
  231.5 12.9 %copy-start.10 = (f32[128,1,256]{2,1,0:T(1,128)S(1)}, f32[128,1,256]{2,1,0:T(1,128)}, u32[]{:S(2)}) copy-start(f32[128,1,256]{2,1,0:T(1,128)} %copy-done.9) | copy-start | bytes 393220
  241.0 77.3 %all-to-all-start.5 = ((bf16[8,128,64]{1,2,0:T(8,128)(2,1)}), bf16[8,128,64]{1,2,0:T(8,128)(2,1)S(1)}, u32[]{:S(2)}, u32[]{:S(2)}) async-start(bf16[8,128,64]{1,2,0:T(8,128)(2,1)} %broadcast_in_dim.44), calls=%async_computation.5 | async-start | bytes 262144 | tf_op jit(solution)/shard_map/all_to_all | solution.py:36
Sparse Core Ops, SparseCore 0:
  9.7 98.7 all-gather.1
  163.7 106.8 reduce-scatter.3
where the time goes:
time: 331 us; the launch traced here: 330 us
  blocking collectives  114 us (34%)
  waiting for transfers between devices  67.2 us (20%)
  matrix products  43.8 us (13%)
  starting transfers between devices  34.4 us (10%)
  other arithmetic  30.8 us (9%)
  local copies, waits for them, and re-layouts  25.9 us (8%)
  between operations  14.4 us (4%)
    psum x1, blocking collectives, body(): gain_sum = lax.psum(grad_gain, ('dp', 'expert'))  72.5 us
    all_gather x1, blocking collectives, body(): router_full = lax.all_gather(router_weight, 'dp', axis=0, tiled=True)  41 us
    all_gather x1, waiting for transfers between devices, in_one_piece(): lax.all_gather(both, axis, axis=dim, tiled=True)  30.4 us
    unnamed x44, local copies, waits for them, and re-layouts  22.4 us
    concatenate x1, other arithmetic, body(): jnp.concatenate([term_gate, term_upper, term_down], axis=1)  21.2 us
    all_to_all x1, waiting for transfers between devices, body(): lax.all_to_all(grad_rows.reshape(window, CAP, D), 'expert', split_axis=0,...  16.8 us
    all_to_all x1, waiting for transfers between devices, body(): lax.all_to_all(produced, 'expert', split_axis=0, concat_axis=0, tiled=True)  14.9 us
    all_to_all x1, starting transfers between devices, body(): lax.all_to_all(outgoing, 'expert', split_axis=0, concat_axis=0, tiled=True)  7.46 us
  transfers between devices with their start and end apart: 8, of which 4 were waited for; matrix products, arithmetic and copies ran while one was open for 14% of the time, Pallas kernels for 0%

commit v1 on v0

--- a/solution.py
+++ b/solution.py
@@ -159,7 +159,7 @@
     grad_router = jnp.dot(hidden.astype(jnp.float32).T, grad_logits, precision=HIGHEST)
     router_part = sum_at_owner(grad_router.astype(jnp.bfloat16), "dp", 0)
     router_mine = over_copies(router_part.astype(jnp.bfloat16), "expert").astype(jnp.float32)
-    gain_sum = lax.psum(grad_gain, ("dp", "expert"))
+    gain_sum = lax.psum(lax.psum(grad_gain, "expert"), "dp")
     grad_gate_out = summed[:, :FF].astype(jnp.bfloat16)[None]
     grad_up_out = summed[:, FF : 2 * FF].astype(jnp.bfloat16)[None]
     grad_down_out = summed[:, 2 * FF :].astype(jnp.bfloat16)[None]

time: 331 us -> 313 us (0.946)
  blocking collectives: 114 us -> 94.8 us
    psum x1 -> x2, blocking collectives: 72.5 us -> 53.8 us  [body(): gain_sum = lax.psum(lax.psum(grad_gain, 'expert'), 'dp')]
  transfers between devices with their start and end apart: 8 -> 8, of which waited for: 4 -> 4; matrix products, arithmetic and copies ran while one was open for 14% -> 15% of each run, Pallas kernels for 0% -> 0%
where the time goes in v1:
time: 313 us; the launch traced here: 311 us
  blocking collectives  94.8 us (30%)
  waiting for transfers between devices  67.2 us (21%)
  matrix products  43.8 us (14%)
  starting transfers between devices  34.4 us (11%)
  other arithmetic  30.8 us (10%)
  local copies, waits for them, and re-layouts  25.9 us (8%)
  between operations  14.4 us (5%)
    psum x2, blocking collectives, body(): gain_sum = lax.psum(lax.psum(grad_gain, 'expert'), 'dp')  53.8 us
    all_gather x1, blocking collectives, body(): router_full = lax.all_gather(router_weight, 'dp', axis=0, tiled=True)  41 us
    all_gather x1, waiting for transfers between devices, in_one_piece(): lax.all_gather(both, axis, axis=dim, tiled=True)  30.4 us
    unnamed x44, local copies, waits for them, and re-layouts  22.4 us
    concatenate x1, other arithmetic, body(): jnp.concatenate([term_gate, term_upper, term_down], axis=1)  21.2 us
    all_to_all x1, waiting for transfers between devices, body(): lax.all_to_all(grad_rows.reshape(window, CAP, D), 'expert', split_axis=0,...  16.8 us
    all_to_all x1, waiting for transfers between devices, body(): lax.all_to_all(produced, 'expert', split_axis=0, concat_axis=0, tiled=True)  14.9 us
    all_to_all x1, starting transfers between devices, body(): lax.all_to_all(outgoing, 'expert', split_axis=0, concat_axis=0, tiled=True)  7.46 us
  transfers between devices with their start and end apart: 8, of which 4 were waited for; matrix products, arithmetic and copies ran while one was open for 15% of the time, Pallas kernels for 0%

profile of v1, /device:TPU:1, one launch (start us, length us, event | category | flops | bytes accessed | tf_op | source)
XLA Modules:
  0.0 311.3 jit_solution(18027880678268970903)
XLA Ops:
  7.3 2.2 pad_maximum_fusion.1
  9.5 0.8 copy.56
  10.4 2.3 reduce-window.6
  13.4 0.7 add_select_fusion
  14.6 1.2 fusion.16
  15.9 2.5 convolution_convert_fusion.3
  18.4 7.5 %all-to-all-start = ((bf16[8,32,2048]{2,1,0:T(8,128)(2,1)}), bf16[8,32,2048]{2,1,0:T(8,128)(2,1)S(1)}, u32[]{:S(2)}, u32[]{:S(2)}) async-start(bf16[8,32,2048]{2,1,0:T(8,128)(2,1)} %bitcast.3), calls=%async_computation | async-start | bytes 2097152 | tf_op jit(solution)/shard_map/all_to_all | solution.py:114
  25.9 41.0 %all_gather.6 = bf16[2048,64]{0,1:T(8,128)(2,1)S(1)} all-gather(bf16[128,64]{0,1:T(8,128)(2,1)S(1)} %copy-done.14), channel_id=1, replica_groups=mesh['dp'=16,'expert'=8] {'dp'}, dimensions={0}, use_global_device_ids=true | all-gather | bytes 278528 | tf_op jit(solution)/shard_map/all_gather | solution.py:97
  67.0 0.7 copy-done.2
  68.2 0.7 fusion.19
  69.0 2.1 convolution_convert_fusion.4
  71.1 6.8 %all-to-all-start.2 = ((bf16[8,32,2048]{2,1,0:T(8,128)(2,1)}), bf16[8,32,2048]{2,1,0:T(8,128)(2,1)S(1)}, u32[]{:S(2)}, u32[]{:S(2)}) async-start(bf16[8,32,2048]{2,1,0:T(8,128)(2,1)} %bitcast.109), calls=%async_computation.2 | async-start | bytes 2097152 | tf_op jit(solution)/shard_map/all_to_all | solution.py:135
  78.1 30.4 %all-gather.2.cloned.1.call-done = bf16[3,2048,1024]{2,1,0:T(8,128)(2,1)} async-done(((bf16[3,128,1024]{2,1,0:T(8,128)(2,1)}), bf16[3,2048,1024]{2,1,0:T(8,128)(2,1)}) %all-gather.2.cloned.1.call-update) | async-done | bytes 12582928 | tf_op jit(solution)/shard_map/all_gather | solution.py:15
  108.5 4.4 %fusion.3 = f32[256,1024]{1,0:T(8,128)} fusion(bf16[256,2048]{1,0:T(8,128)(2,1)S(1)} %bitcast.100, bf16[3,2048,1024]{2,1,0:T(8,128)(2,1)} %all-gather.2.cloned.1.call-done), kind=kOutput, calls=%fused_computation.10 | convolution fusion | flops 1073741824 | bytes 6291456 | tf_op jit(solution)/shard_map/dot_general | solution.py:71
  112.9 4.4 %fusion.1 = f32[256,1024]{1,0:T(8,128)} fusion(bf16[256,2048]{1,0:T(8,128)(2,1)S(1)} %bitcast.101, bf16[3,2048,1024]{2,1,0:T(8,128)(2,1)} %all-gather.2.cloned.1.call-done), kind=kOutput, calls=%fused_computation.8 | convolution fusion | flops 1073741824 | bytes 6291456 | tf_op jit(solution)/shard_map/dot_general | solution.py:70
  117.3 4.4 %multiply_convert_fusion = (bf16[256,1024]{1,0:T(8,128)(2,1)S(1)}, bf16[256,1024]{1,0:T(8,128)(2,1)S(1)}, bf16[256,1024]{1,0:T(8,128)(2,1)S(1)}) fusion(f32[256,1024]{1,0:T(8,128)} %fusion.1, f32[256,1024]{1,0:T(8,128)} %fusion.3, bf16[256,2048]{1,0:T(8,128)(2,1)S(1)} %bitcast.104, bf16[3,2048,1024]{2,1,0:T(8,128)(2,1)} %all-gather.2.cloned.1.call-done), kind=kOutput, calls=%fused_computation.36 | convolution fusion | flops 1077936128 | bytes 8912896 | tf_op jit(solution)/shard_map/dot_general | solution.py:80
  121.7 1.3 convolution_convert_fusion
  123.1 1.3 convolution_convert_fusion.1
  124.4 1.3 convolution_convert_fusion.2
  125.7 21.2 %pad_maximum_fusion = bf16[2048,3072]{0,1:T(8,128)(2,1)} fusion(bf16[2048,1024]{0,1:T(8,128)(2,1)S(1)} %convolution_convert_fusion, bf16[2048,1024]{0,1:T(8,128)(2,1)S(1)} %convolution_convert_fusion.1, bf16[2048,1024]{0,1:T(8,128)(2,1)S(1)} %convolution_convert_fusion.2), kind=kLoop, calls=%fused_computation | loop fusion | flops 37748736 | bytes 25165824 | tf_op jit(solution)/shard_map/concatenate | solution.py:148
  146.9 16.6 %copy.68 = bf16[2048,3072]{1,0:T(8,128)(2,1)} copy(bf16[2048,3072]{0,1:T(8,128)(2,1)} %pad_maximum_fusion) | data formatting | bytes 25165824
  163.6 1.0 copy-done.8
  164.6 4.6 %fusion.8 = bf16[256,2048]{1,0:T(8,128)(2,1)} fusion(bf16[256,1024]{1,0:T(8,128)(2,1)S(1)} %copy-done.8, bf16[3,2048,1024]{2,1,0:T(8,128)(2,1)} %all-gather.2.cloned.1.call-done), kind=kOutput, calls=%fused_computation.17 | convolution fusion | flops 1074266112 | bytes 5767168 | tf_op jit(solution)/shard_map/dot_general | solution.py:73
  169.2 6.1 %all-to-all-start.1 = ((bf16[8,32,2048]{2,1,0:T(8,128)(2,1)}), bf16[8,32,2048]{2,1,0:T(8,128)(2,1)S(1)}, u32[]{:S(2)}, u32[]{:S(2)}) async-start(bf16[8,32,2048]{2,1,0:T(8,128)(2,1)} %bitcast.8), calls=%async_computation.1 | async-start | bytes 2097152 | tf_op jit(solution)/shard_map/all_to_all | solution.py:121
  175.3 3.5 %fusion = f32[256,2048]{1,0:T(8,128)S(1)} fusion(bf16[256,1024]{1,0:T(8,128)(2,1)S(1)} %copy-done.6, bf16[3,2048,1024]{2,1,0:T(8,128)(2,1)} %all-gather.2.cloned.1.call-done), kind=kOutput, calls=%fused_computation.7 | convolution fusion | flops 1073741824 | bytes 6815744 | tf_op jit(solution)/shard_map/dot_general | solution.py:85
  178.9 4.5 %fusion.7 = bf16[256,2048]{1,0:T(8,128)(2,1)} fusion(f32[256,2048]{1,0:T(8,128)S(1)} %fusion, bf16[256,1024]{1,0:T(8,128)(2,1)S(1)} %copy-done.4, bf16[3,2048,1024]{2,1,0:T(8,128)(2,1)} %all-gather.2.cloned.1.call-done), kind=kOutput, calls=%fused_computation.16 | convolution fusion | flops 1074790400 | bytes 7864320 | tf_op jit(solution)/shard_map/dot_general | solution.py:87
  183.4 14.9 %all-to-all-done.1 = bf16[8,32,2048]{2,1,0:T(8,128)(2,1)S(1)} async-done(((bf16[8,32,2048]{2,1,0:T(8,128)(2,1)}), bf16[8,32,2048]{2,1,0:T(8,128)(2,1)S(1)}, u32[]{:S(2)}, u32[]{:S(2)}) %all-to-all-start.1) | async-done | bytes 1048608 | tf_op jit(solution)/shard_map/all_to_all | solution.py:121
  198.3 3.6 %all-to-all-start.3 = ((bf16[8,32,2048]{2,1,0:T(8,128)(2,1)}), bf16[8,32,2048]{2,1,0:T(8,128)(2,1)S(1)}, u32[]{:S(2)}, u32[]{:S(2)}) async-start(bf16[8,32,2048]{2,1,0:T(8,128)(2,1)} %bitcast.110), calls=%async_computation.3 | async-start | bytes 2097152 | tf_op jit(solution)/shard_map/all_to_all | solution.py:141
  201.8 0.5 fusion.9
  202.4 3.6 %fusion.18 = f32[1,128,8]{2,0,1:T(1,128)S(1)} fusion(f32[256,1,1]{0,1,2:T(1,128)S(1)} %bitcast.115, s32[128,8]{1,0:T(8,128)S(1)} %copy.59), kind=kOutput, calls=%fused_computation.42 | convolution fusion | flops 3407872 | bytes 9216 | tf_op jit(solution)/shard_map/tks,s->tk/dot_general | solution.py:128
  206.2 0.5 fusion.12
  206.8 0.8 copy.86
  207.6 16.8 %all-to-all-done.3 = bf16[8,32,2048]{2,1,0:T(8,128)(2,1)S(1)} async-done(((bf16[8,32,2048]{2,1,0:T(8,128)(2,1)}), bf16[8,32,2048]{2,1,0:T(8,128)(2,1)S(1)}, u32[]{:S(2)}, u32[]{:S(2)}) %all-to-all-start.3) | async-done | bytes 1048608 | tf_op jit(solution)/shard_map/all_to_all | solution.py:141
  224.4 6.8 %all-to-all-start.4 = ((bf16[16,128,64]{1,2,0:T(8,128)(2,1)}), bf16[16,128,64]{1,2,0:T(8,128)(2,1)S(1)}, u32[]{:S(2)}, u32[]{:S(2)}) async-start(bf16[16,128,64]{1,2,0:T(8,128)(2,1)} %bitcast.98), calls=%async_computation.4 | async-start | bytes 524288 | tf_op jit(solution)/shard_map/all_to_all | solution.py:30
  231.5 1.9 fusion.14
  233.4 0.6 multiply_multiply_fusion
  234.1 1.1 fusion.15
  235.2 5.1 %all-to-all-done.4 = bf16[16,128,64]{1,2,0:T(8,128)(2,1)S(1)} async-done(((bf16[16,128,64]{1,2,0:T(8,128)(2,1)}), bf16[16,128,64]{1,2,0:T(8,128)(2,1)S(1)}, u32[]{:S(2)}, u32[]{:S(2)}) %all-to-all-start.4) | async-done | bytes 262176 | tf_op jit(solution)/shard_map/all_to_all | solution.py:30
  240.3 0.7 broadcast_in_dim.44
  241.0 3.4 %all-to-all-start.5 = ((bf16[8,128,64]{1,2,0:T(8,128)(2,1)}), bf16[8,128,64]{1,2,0:T(8,128)(2,1)S(1)}, u32[]{:S(2)}, u32[]{:S(2)}) async-start(bf16[8,128,64]{1,2,0:T(8,128)(2,1)} %broadcast_in_dim.44), calls=%async_computation.5 | async-start | bytes 262144 | tf_op jit(solution)/shard_map/all_to_all | solution.py:36
  244.4 1.4 convolution_convert_fusion.5
  245.8 21.3 %psum.14 = f32[2048]{0:T(1024)S(1)} all-reduce(f32[2048]{0:T(1024)S(1)} %get-tuple-element.42), channel_id=1, replica_groups=mesh['dp'=16,'expert'=8] {'expert'}, use_global_device_ids=true, to_apply=%region_12.13 | all-reduce | flops 2048 | bytes 16384 | tf_op jit(solution)/shard_map/psum | solution.py:162
  267.1 32.5 %psum.15 = f32[2048]{0:T(1024)} all-reduce(f32[2048]{0:T(1024)S(1)} %psum.14), channel_id=1, replica_groups=mesh['dp'=16,'expert'=8] {'dp'}, use_global_device_ids=true, to_apply=%region_13.14 | all-reduce | flops 2048 | bytes 16384 | tf_op jit(solution)/shard_map/psum | solution.py:162
  299.6 0.6 convert_reduce_fusion.1
  300.2 1.2 fusion.43
  301.6 0.9 copy.64
  302.6 0.9 copy.63
  303.6 0.9 copy.62
  (70 shorter events, 3.4 us)
Async XLA Ops:
  7.2 61.8 %copy-start = (bf16[128,2048]{1,0:T(8,128)(2,1)S(1)}, bf16[128,2048]{1,0:T(8,128)(2,1)}, u32[]{:S(2)}) copy-start(bf16[128,2048]{1,0:T(8,128)(2,1)} %param.15) | copy-start | bytes 1572868
  7.2 60.9 %copy-start.13 = (s32[128,8]{0,1:T(8,128)S(1)}, s32[128,8]{0,1:T(8,128)}, u32[]{:S(2)}) copy-start(s32[128,8]{0,1:T(8,128)} %param.11) | copy-start | bytes 12292
  7.2 60.5 %copy-start.1 = (bf16[128,2048]{1,0:T(8,128)(2,1)S(1)}, bf16[128,2048]{1,0:T(8,128)(2,1)}, u32[]{:S(2)}) copy-start(bf16[128,2048]{1,0:T(8,128)(2,1)} %param.8) | copy-start | bytes 1572868
  7.2 60.5 %copy-start.12 = (f32[2048]{0:T(1024)S(1)}, f32[2048]{0:T(1024)}, u32[]{:S(2)}) copy-start(f32[2048]{0:T(1024)} %param.9) | copy-start | bytes 24580
  7.2 18.7 %copy-start.14 = (bf16[128,64]{0,1:T(8,128)(2,1)S(1)}, bf16[128,64]{0,1:T(8,128)(2,1)}, u32[]{:S(2)}) copy-start(bf16[128,64]{0,1:T(8,128)(2,1)} %param.10) | copy-start | bytes 49156
  7.2 101.3 %all-gather.2.cloned.1.call-start = ((), (), s32[]{:S(2)}) async-start(), calls=%async_computation.7 | async-start | bytes 13369344 | tf_op jit(solution)/shard_map/all_gather | solution.py:15
  15.9 10.0 %copy-start.17 = (f32[128]{0:T(128)}, f32[128]{0:T(128)S(1)}, u32[]{:S(2)}) copy-start(f32[128]{0:T(128)S(1)} %fusion.16) | copy-start | bytes 1540
  15.9 190.3 %copy-start.15 = (f32[128]{0:T(128)}, f32[128]{0:T(128)S(1)}, u32[]{:S(2)}) copy-start(f32[128]{0:T(128)S(1)} %fusion.34) | copy-start | bytes 1540
  18.4 52.6 %all-to-all-start = ((bf16[8,32,2048]{2,1,0:T(8,128)(2,1)}), bf16[8,32,2048]{2,1,0:T(8,128)(2,1)S(1)}, u32[]{:S(2)}, u32[]{:S(2)}) async-start(bf16[8,32,2048]{2,1,0:T(8,128)(2,1)} %bitcast.3), calls=%async_computation | async-start | bytes 2097152 | tf_op jit(solution)/shard_map/all_to_all | solution.py:114
  67.0 0.7 copy-start.2
  69.0 2.1 copy-start.9
  71.1 46.3 %all-to-all-start.2 = ((bf16[8,32,2048]{2,1,0:T(8,128)(2,1)}), bf16[8,32,2048]{2,1,0:T(8,128)(2,1)S(1)}, u32[]{:S(2)}, u32[]{:S(2)}) async-start(bf16[8,32,2048]{2,1,0:T(8,128)(2,1)} %bitcast.109), calls=%async_computation.2 | async-start | bytes 2097152 | tf_op jit(solution)/shard_map/all_to_all | solution.py:135
  77.9 222.3 %reduce-scatter.4.cloned.1.call-start = ((), (), s32[]{:S(2)}) async-start(), calls=%async_computation.8 | async-start | bytes 13369344
  121.7 1.4 copy-start.7
  121.7 1.4 copy-start.3
  121.7 2.7 copy-start.5
  163.5 1.0 copy-start.8
  164.6 10.7 %copy-start.6 = (bf16[256,1024]{1,0:T(8,128)(2,1)S(1)}, bf16[256,1024]{1,0:T(8,128)(2,1)}, u32[]{:S(2)}) copy-start(bf16[256,1024]{1,0:T(8,128)(2,1)} %copy-done.5) | copy-start | bytes 1572868
  169.2 29.1 %all-to-all-start.1 = ((bf16[8,32,2048]{2,1,0:T(8,128)(2,1)}), bf16[8,32,2048]{2,1,0:T(8,128)(2,1)S(1)}, u32[]{:S(2)}, u32[]{:S(2)}) async-start(bf16[8,32,2048]{2,1,0:T(8,128)(2,1)} %bitcast.8), calls=%async_computation.1 | async-start | bytes 2097152 | tf_op jit(solution)/shard_map/all_to_all | solution.py:121
  175.3 3.5 %copy-start.4 = (bf16[256,1024]{1,0:T(8,128)(2,1)S(1)}, bf16[256,1024]{1,0:T(8,128)(2,1)}, u32[]{:S(2)}) copy-start(bf16[256,1024]{1,0:T(8,128)(2,1)} %copy-done.3) | copy-start | bytes 1572868
  198.3 26.1 %all-to-all-start.3 = ((bf16[8,32,2048]{2,1,0:T(8,128)(2,1)}), bf16[8,32,2048]{2,1,0:T(8,128)(2,1)S(1)}, u32[]{:S(2)}, u32[]{:S(2)}) async-start(bf16[8,32,2048]{2,1,0:T(8,128)(2,1)} %bitcast.110), calls=%async_computation.3 | async-start | bytes 2097152 | tf_op jit(solution)/shard_map/all_to_all | solution.py:141
  206.2 0.6 copy-start.11
  224.4 15.9 %all-to-all-start.4 = ((bf16[16,128,64]{1,2,0:T(8,128)(2,1)}), bf16[16,128,64]{1,2,0:T(8,128)(2,1)S(1)}, u32[]{:S(2)}, u32[]{:S(2)}) async-start(bf16[16,128,64]{1,2,0:T(8,128)(2,1)} %bitcast.98), calls=%async_computation.4 | async-start | bytes 524288 | tf_op jit(solution)/shard_map/all_to_all | solution.py:30
  231.2 2.9 copy-start.16
  231.5 12.9 %copy-start.10 = (f32[128,1,256]{2,1,0:T(1,128)S(1)}, f32[128,1,256]{2,1,0:T(1,128)}, u32[]{:S(2)}) copy-start(f32[128,1,256]{2,1,0:T(1,128)} %copy-done.9) | copy-start | bytes 393220
  241.0 58.6 %all-to-all-start.5 = ((bf16[8,128,64]{1,2,0:T(8,128)(2,1)}), bf16[8,128,64]{1,2,0:T(8,128)(2,1)S(1)}, u32[]{:S(2)}, u32[]{:S(2)}) async-start(bf16[8,128,64]{1,2,0:T(8,128)(2,1)} %broadcast_in_dim.44), calls=%async_computation.5 | async-start | bytes 262144 | tf_op jit(solution)/shard_map/all_to_all | solution.py:36
Sparse Core Ops, SparseCore 0:
  9.7 98.7 all-gather.1
  163.7 107.3 reduce-scatter.3
